TPU v7x, 32 devices: a whole 2x2x4 slice. The times are simulated.
32 devices in a mesh: gr: 8 (over z, core), gc: 4 (over y, x).
Axes of the slice: x: 2, y: 2, z: 4, core: 2. Of those that a mesh axis runs over, the one named last changes fastest.
Arguments:
- projectors: bfloat16 [2, 8192, 9216], P(None, ('gr', 'gc')), may hold values from -0.0625 to 0.0625
- wavefunctions: bfloat16 [2, 8192, 512], P(None, ('gr', 'gc')), may hold values from -6 to 6
- coupling: float32 [512, 18, 18], P('gc'), may hold values from -1.5 to 1.5
- atom_order: int32 [512], replicated, may hold values from 0 to 511, each once
Outputs:
- coupled: float32 [9216, 512], P('gc', 'gr')
Inputs may be any that keep to these rules, and one draw needn't show every extreme that they name: `atom_order`: a permutation of the atoms.
All inputs are finite; a program needn't handle non-finite values.
Results may differ from a plain program's by a relative error of at most 0.0003.
Values sent between devices are 32-bit elements; how exact they have to be, the bound alone decides.
A program may use at most 128 MiB of HBM per device.

v0:
```python
import jax
import jax.numpy as jnp
from jax import lax
from jax.sharding import PartitionSpec as P

ATOMS = 512
NH = 18
BANDS = 512
NKB = 9216


def shards(projectors, wavefunctions, coupling, atom_order):
    rows_here = projectors.shape[1]
    shaped = projectors.reshape(2, rows_here, ATOMS, NH)
    waves = wavefunctions.reshape(2 * rows_here, BANDS)
    owned_slots = NKB // lax.axis_size("gc")
    columns = jnp.take(shaped, atom_order, axis=2).reshape(
        2 * rows_here, owned_slots * lax.axis_size("gc")
    )
    term = lax.dot_general(
        columns, waves, (((0,), (0,)), ((), ())), preferred_element_type=jnp.float32
    )
    partial_rows = lax.psum_scatter(2.0 * term, "gc", scatter_dimension=0, tiled=True)
    becp = lax.psum_scatter(partial_rows, "gr", scatter_dimension=1, tiled=True)
    local_atoms = coupling.shape[0]
    becp = becp.reshape(local_atoms, NH, becp.shape[1])
    coupled = jnp.einsum("kij,kjb->kib", coupling, becp, precision=lax.Precision.HIGHEST)
    return coupled.reshape(local_atoms * NH, becp.shape[2])


def solution(mesh):
    return jax.shard_map(
        shards,
        mesh=mesh,
        in_specs=(
            P(None, ("gr", "gc"), None),
            P(None, ("gr", "gc"), None),
            P("gc", None, None),
            P(),
        ),
        out_specs=P("gc", "gr"),
        check_vma=False,
    )
```

profile of v0, /device:TPU:0, one launch (start us, length us, event | category | flops | bytes accessed | tf_op | source)
XLA Modules:
  0.0 341.5 jit_solution(17600549290242266656)
XLA Ops:
  6.5 0.0 copy-start
  6.5 0.0 reduce-scatter.5.cloned.1.call-start
  6.5 0.7 compare_select_fusion
  7.3 0.7 compare_and_fusion
  8.0 23.5 %copy.10 = bf16[2,256,9216]{1,0,2:T(2,128)(2,1)} copy(bf16[2,256,9216]{2,1,0:T(8,128)(2,1)} %param.4) | data formatting | bytes 18874368 | tf_op args[0]
  31.5 32.8 %gather_fusion = bf16[512,2,256,18]{2,1,3,0:T(2,128)(2,1)} fusion(bf16[2,256,512,18]{1,0,3,2:T(2,128)(2,1)} %bitcast.17, s32[1024]{0:T(1024)S(1)} %pad_clamp_fusion), kind=kCustom, calls=%fused_computation | custom fusion | bytes 18876416 | tf_op jit(solution)/shard_map/jit(_take)/gather | solution.py:17
  64.3 13.2 %broadcast_select_fusion = bf16[512,2,256,18]{2,1,3,0:T(2,128)(2,1)S(1)} fusion(bf16[512,2,256,18]{2,1,3,0:T(2,128)(2,1)} %gather_fusion, pred[512]{0:T(512)(128)(4,1)S(1)} %compare_and_fusion), kind=kLoop, calls=%fused_computation.1 | loop fusion | flops 4718592 | bytes 18874880 | tf_op jit(solution)/shard_map/jit(_take)/select_n | solution.py:17
  77.5 2.8 copy.15
  80.3 0.0 copy-done
  80.3 9.1 %convolution_multiply_fusion = f32[9216,512]{1,0:T(8,128)} fusion(bf16[512,9216]{0,1:T(8,128)(2,1)S(1)} %bitcast.18, bf16[512,512]{1,0:T(8,128)(2,1)S(1)} %bitcast.16), kind=kOutput, calls=%fused_computation.2 | convolution fusion | flops 4836556800 | bytes 28835840 | tf_op jit(solution)/shard_map/dot_general | solution.py:20
  89.4 0.0 reduce-scatter.5.cloned.1.call-update
  89.4 0.0 copy-start.1
  89.4 0.0 reduce-scatter.7.cloned.1.call-start
  89.4 173.6 %reduce-scatter.5.cloned.1.call-done = f32[2304,512]{1,0:T(8,128)} async-done(((f32[9216,512]{1,0:T(8,128)}), f32[2304,512]{1,0:T(8,128)}) %reduce-scatter.5.cloned.1.call-update) | async-done | bytes 4718608 | tf_op jit(solution)/shard_map/reduce_scatter | solution.py:23
  263.0 6.1 %copy.13 = f32[2304,512]{0,1:T(8,128)} copy(f32[2304,512]{1,0:T(8,128)} %reduce-scatter.5.cloned.1.call-done) | data formatting | bytes 9437184
  269.1 0.0 reduce-scatter.7.cloned.1.call-update
  269.1 0.0 copy-done.1
  269.1 0.6 copy.11
  269.7 54.5 %reduce-scatter.7.cloned.1.call-done = f32[64,2304]{1,0:T(8,128)} async-done(((f32[512,2304]{1,0:T(8,128)}), f32[64,2304]{1,0:T(8,128)}) %reduce-scatter.7.cloned.1.call-update) | async-done | bytes 589840
  324.2 1.4 copy.14
  325.6 1.3 reshape.52
  326.9 5.2 %convolution_bitcast_fusion = f32[128,18,64]{2,1,0:T(8,128)} fusion(f32[128,18,64]{2,1,0:T(8,128)} %reshape.52, f32[128,18,18]{2,1,0:T(8,128)S(1)} %copy.11), kind=kOutput, calls=%fused_computation.3 | convolution fusion | flops 31850496 | bytes 1345536 | tf_op jit(solution)/shard_map/kij,kjb->kib/dot_general | solution.py:27
  332.1 1.4 reshape.53
  333.5 1.2 copy.12
  (1 shorter events, 0.0 us)
Async XLA Ops:
  6.5 73.7 %copy-start = (bf16[2,256,512]{2,1,0:T(8,128)(2,1)S(1)}, bf16[2,256,512]{2,1,0:T(8,128)(2,1)}, u32[]{:S(2)}) copy-start(bf16[2,256,512]{2,1,0:T(8,128)(2,1)} %param.5) | copy-start | bytes 1572868
  6.5 256.5 %reduce-scatter.5.cloned.1.call-start = ((), (), s32[]{:S(2)}) async-start(), calls=%async_computation.2 | async-start | bytes 23592960 | tf_op jit(solution)/shard_map/reduce_scatter | solution.py:23
  89.4 179.7 %copy-start.1 = (f32[128,18,18]{0,2,1:T(8,128)S(1)}, f32[128,18,18]{0,2,1:T(8,128)}, u32[]{:S(2)}) copy-start(f32[128,18,18]{0,2,1:T(8,128)} %param.6) | copy-start | bytes 497668
  89.4 234.8 %reduce-scatter.7.cloned.1.call-start = ((), (), s32[]{:S(2)}) async-start(), calls=%async_computation.3 | async-start | bytes 5308416
Sparse Core Ops, SparseCore 0:
  89.5 173.4 reduce-scatter.4
  269.2 54.8 reduce-scatter.6
where the time goes:
time: 342 us
  waiting for transfers between devices  228 us (67%)
  local copies, waits for them, and re-layouts  71 us (21%)
  other arithmetic  14.7 us (4%)
  matrix products  14.3 us (4%)
  between operations  13.5 us (4%)
    reduce_scatter x1, waiting for transfers between devices, shards(): lax.psum_scatter(2.0 * term, 'gc', scatter_dimension=0, tiled=True)  174 us
    unnamed x3, waiting for transfers between devices  54.5 us
    unnamed x9, local copies, waits for them, and re-layouts  34.3 us
    gather x1, local copies, waits for them, and re-layouts, shards(): jnp.take(shaped, atom_order, axis=2)  32.8 us
    select_n x2, other arithmetic, shards(): jnp.take(shaped, atom_order, axis=2)  14 us
    dot_general x1, matrix products, shards(): lax.dot_general(columns, waves, (((0,), (0,)), ((), ())), preferred_eleme...  9.09 us
  transfers between devices with their start and end apart: 2, of which 2 were waited for; matrix products, arithmetic and copies ran while one was open for 0% of the time, Pallas kernels for 0%

commit v1 on v0

v1 whole, which is shorter than its diff:
```python
import functools
import math

import jax
import jax.numpy as jnp
from jax import lax
from jax.experimental import pallas as pl
from jax.experimental.pallas import tpu as pltpu
from jax.sharding import PartitionSpec as P

MESH = pl.DeviceIdType.MESH
GROUP = 4
LANES = 128


def plain(projectors, wavefunctions, coupling, atom_order):
    rows_here, nkb = projectors.shape[1:]
    bands = wavefunctions.shape[2]
    atoms = atom_order.shape[0]
    nh = nkb // atoms
    shaped = projectors.reshape(2, rows_here, atoms, nh)
    waves = wavefunctions.reshape(2 * rows_here, bands)
    columns = jnp.take(shaped, atom_order, axis=2).reshape(2 * rows_here, nkb)
    term = lax.dot_general(columns, waves, (((0,), (0,)), ((), ())), preferred_element_type=jnp.float32)
    partial_rows = lax.psum_scatter(2.0 * term, "gc", scatter_dimension=0, tiled=True)
    becp = lax.psum_scatter(partial_rows, "gr", scatter_dimension=1, tiled=True)
    local_atoms = coupling.shape[0]
    becp = becp.reshape(local_atoms, nh, becp.shape[1])
    coupled = jnp.einsum("kij,kjb->kib", coupling, becp, precision=lax.Precision.HIGHEST)
    return coupled.reshape(local_atoms * nh, becp.shape[2])


def path_of(column):
    first, other = ("A", "B") if column % 2 == 0 else ("B", "A")
    order = (first, other, "Z") if (column // 2) % 3 == 1 else (first, "Z", other)
    return order, (1 if column % 2 == 0 else -1)


def kernel(size, nh, apo, columns, order_ref, term_ref, coup_ref, out_ref, nat, acc, oth, rec, nat_sem, send_sem, recv_sem):
    gr, gc = lax.axis_index("gr"), lax.axis_index("gc")
    core, z = lax.rem(gr, 2), gr // 2
    me = {"A": gc // size["B"], "B": lax.rem(gc, size["B"]), "Z": z}
    half = apo // 2

    loads = [
        pltpu.make_async_copy(term_ref.at[:, pl.ds(i * LANES, LANES)], nat.at[i], nat_sem.at[i])
        for i in range(size["Z"])
    ]
    for load in loads:
        load.start()

    def neighbour(dim, way):
        n = size[dim]
        place = lax.rem(me[dim] + n + way, n)
        if dim == "A":
            return {"gr": gr, "gc": place * size["B"] + me["B"]}
        if dim == "B":
            return {"gr": gr, "gc": me["A"] * size["B"] + place}
        return {"gr": place * 2 + core, "gc": gc}

    partner = {"gr": gr + 1 - 2 * core, "gc": gc}
    greeted = [partner]
    for dim in ("A", "B", "Z"):
        if size[dim] > 1:
            greeted.append(neighbour(dim, 1))
        if size[dim] > 2:
            greeted.append(neighbour(dim, -1))
    barrier = pltpu.get_barrier_semaphore()
    for device in greeted:
        pl.semaphore_signal(barrier, inc=1, device_id=device, device_id_type=MESH)
    pl.semaphore_wait(barrier, len(greeted))

    for load in loads:
        load.wait()

    def copy(src, dst, column, slot, device):
        return pltpu.make_async_remote_copy(
            src_ref=src, dst_ref=dst, send_sem=send_sem.at[column, slot], recv_sem=recv_sem.at[column, slot],
            device_id=device, device_id_type=MESH,
        )

    def pack(dst, which, column):
        path, _ = path_of(column)

        def body(owner, carry):
            at = {"A": owner // size["B"], "B": lax.rem(owner, size["B"])}
            for i in range(GROUP):
                row = order_ref[owner * apo + which * half + column * GROUP + i] * nh
                for zz in range(size["Z"]):
                    at["Z"] = zz
                    where = tuple(at[d] for d in path)
                    dst[where + (pl.ds(i * nh, nh), slice(None))] = nat[zz, pl.ds(row, nh), :]
            return carry

        lax.fori_loop(0, size["A"] * size["B"], body, 0)

    def add(dst, prefix, src, src_prefix, rest):
        def body(t, carry):
            where = []
            for n in reversed(rest):
                where.insert(0, lax.rem(t, n))
                t = t // n
            where = tuple(where)
            dst[tuple(prefix) + where] = dst[tuple(prefix) + where] + src[tuple(src_prefix) + where]
            return carry

        if rest:
            lax.fori_loop(0, math.prod(rest), body, 0)
        else:
            dst[tuple(prefix)] = dst[tuple(prefix)] + src[tuple(src_prefix)]

    def steps_of(column):
        path, way = path_of(column)
        found = []
        for stage, dim in enumerate(path):
            n = size[dim]
            turn = way if dim == "Z" else 1
            fixed = [me[d] for d in path[:stage]]
            rest = [size[d] for d in path[stage + 1:]]
            for t in range(n - 1):
                sent = lax.rem(me[dim] - turn * (t + 1) + 2 * n, n)
                got = lax.rem(me[dim] - turn * (t + 2) + 2 * n, n)
                found.append((stage, t, fixed + [sent], fixed + [got], rest, neighbour(dim, turn)))
        return found

    started = {}

    def begin(column, slot, made):
        started[column, slot] = made
        made.start()

    def send_step(column, number):
        stage, t, sent, _, _, device = steps[column][number]
        begin(column, number + 1, copy(acc[column].at[tuple(sent)], rec[column][stage + 1].at[t], column, number + 1, device))

    steps = [steps_of(c) for c in range(columns)]
    n_steps = len(steps[0])

    def phase(number, c):
        if number == 0:
            pack(oth[c], 1 - core, c)
            begin(c, 0, copy(oth[c], rec[c][0], c, 0, partner))
            pack(acc[c], core, c)
            return
        started[c, number - 1].wait_recv()
        if number == 1:
            path, _ = path_of(c)
            add(acc[c], (), rec[c][0], (), [size[d] for d in path])
        else:
            stage, t, _, got, rest, _ = steps[c][number - 2]
            add(acc[c], got, rec[c][stage + 1], [t], rest)
        if number <= n_steps:
            send_step(c, number - 1)
            return
        path, _ = path_of(c)
        mine = tuple(me[d] for d in path)
        for i in range(GROUP):
            becp = 2.0 * acc[c][mine + (pl.ds(i * nh, nh), slice(None))]
            out_ref[core, c, pl.ds(i * nh, nh), :] = jnp.dot(
                coup_ref[core * half + c * GROUP + i], becp,
                precision=lax.Precision.HIGHEST, preferred_element_type=jnp.float32,
            )
        begin(c, n_steps + 1, copy(out_ref.at[core, c], out_ref.at[core, c], c, n_steps + 1, partner))

    lag = [0, 1] + [2 * i + 1 for i in range(1, n_steps + 1)]
    for tick in range(columns + lag[-1]):
        for number in reversed(range(n_steps + 2)):
            c = tick - lag[number]
            if 0 <= c < columns:
                phase(number, c)
    for c in range(columns):
        started[c, n_steps + 1].wait_recv()
        for slot in range(n_steps + 2):
            started[c, slot].wait_send()


def routed(size, projectors, wavefunctions, coupling, atom_order):
    rows_here, nkb = projectors.shape[1:]
    bands = wavefunctions.shape[2]
    atoms = atom_order.shape[0]
    nh, apo = nkb // atoms, coupling.shape[0]
    columns = apo // 2 // GROUP
    n_steps = sum(size.values()) - 3
    tile = (GROUP * nh, LANES)
    term = lax.dot_general(
        projectors.reshape(2 * rows_here, nkb), wavefunctions.reshape(2 * rows_here, bands),
        (((0,), (0,)), ((), ())), preferred_element_type=jnp.float32,
    )
    acc, rec = [], []
    for c in range(columns):
        n1, n2, n3 = (size[d] for d in path_of(c)[0])
        acc.append(pltpu.VMEM((n1, n2, n3) + tile, jnp.float32))
        rec.append([
            pltpu.VMEM((n1, n2, n3) + tile, jnp.float32),
            pltpu.VMEM((n1 - 1, n2, n3) + tile, jnp.float32),
            pltpu.VMEM((n2 - 1, n3) + tile, jnp.float32),
            pltpu.VMEM((n3 - 1,) + tile, jnp.float32),
        ])
    out = pl.pallas_call(
        functools.partial(kernel, size, nh, apo, columns),
        out_shape=jax.ShapeDtypeStruct((2, columns) + tile, jnp.float32),
        in_specs=[
            pl.BlockSpec(memory_space=pltpu.SMEM),
            pl.BlockSpec(memory_space=pl.ANY),
            pl.BlockSpec(memory_space=pltpu.VMEM),
        ],
        out_specs=pl.BlockSpec(memory_space=pltpu.VMEM),
        scratch_shapes=[
            pltpu.VMEM((size["Z"], nkb, LANES), jnp.float32),
            acc,
            list(acc),
            rec,
            pltpu.SemaphoreType.DMA((size["Z"],)),
            pltpu.SemaphoreType.DMA((columns, n_steps + 2)),
            pltpu.SemaphoreType.DMA((columns, n_steps + 2)),
        ],
        compiler_params=pltpu.CompilerParams(
            collective_id=0, has_side_effects=True, vmem_limit_bytes=67_043_328
        ),
    )(atom_order, term, coupling)
    out = out.reshape(apo * nh, LANES)
    own = LANES // 2
    return jnp.where(lax.rem(lax.axis_index("gr"), 2) == 0, out[:, :own], out[:, own:])


def solution(mesh):
    gr, gc = mesh.shape["gr"], mesh.shape["gc"]
    wide = max(d for d in range(1, math.isqrt(gc) + 1) if gc % d == 0)
    size = {"A": wide, "B": gc // wide, "Z": gr // 2}

    def shards(projectors, wavefunctions, coupling, atom_order):
        fits = (
            gr % 2 == 0
            and min(size.values()) > 1
            and wavefunctions.shape[2] == size["Z"] * LANES
            and coupling.shape[0] % (2 * GROUP) == 0
        )
        if fits:
            return routed(size, projectors, wavefunctions, coupling, atom_order)
        return plain(projectors, wavefunctions, coupling, atom_order)

    return jax.shard_map(
        shards,
        mesh=mesh,
        in_specs=(
            P(None, ("gr", "gc"), None),
            P(None, ("gr", "gc"), None),
            P("gc", None, None),
            P(),
        ),
        out_specs=P("gc", "gr"),
        check_vma=False,
    )
```

time: 342 us -> 122 us (0.36)
  waiting for transfers between devices: 228 us -> 0 us
  Pallas kernels: 0 us -> 104 us
  local copies, waits for them, and re-layouts: 71 us -> 4.35 us
  other arithmetic: 14.7 us -> 0.88 us
  between operations: 13.5 us -> 0.04 us
    reduce_scatter x1 -> x0, waiting for transfers between devices: 174 us -> none  [shards(): lax.psum_scatter(2.0 * term, 'gc', scatter_dimension=0, tiled=True)]
    pallas_call x0 -> x1, Pallas kernels: none -> 104 us  [routed(): pl.pallas_call(functools.partial(kernel, size, nh, apo, columns), out_sha...]
    unnamed x3 -> x0, waiting for transfers between devices: 54.5 us -> none
    gather x1 -> x0, local copies, waits for them, and re-layouts: 32.8 us -> none  [shards(): jnp.take(shaped, atom_order, axis=2)]
    unnamed x9 -> x5, local copies, waits for them, and re-layouts: 34.3 us -> 2.36 us
    select_n x2 -> x1, other arithmetic: 14 us -> 0.88 us  [routed(): jnp.where(lax.rem(lax.axis_index('gr'), 2) == 0, out[:, :own], out[:, own:])]
    reshape x3 -> x0, local copies, waits for them, and re-layouts: 3.88 us -> none  [the longest x2 2.6 us: shards(): return coupled.reshape(local_atoms * NH, becp.shape[2])]
    dot_general x2 -> x1, matrix products: 14.3 us -> 11.6 us  [routed(): lax.dot_general(projectors.reshape(2 * rows_here, nkb), wavefunctions.res...]
  transfers between devices with their start and end apart: 2 -> 0, of which waited for: 2 -> 0; matrix products, arithmetic and copies ran while one was open for 0% -> 0% of each run, Pallas kernels for 0% -> 0%
where the time goes in v1:
time: 122 us; the launch traced here: 121 us
  Pallas kernels  104 us (85%)
  matrix products  11.6 us (10%)
  local copies, waits for them, and re-layouts  4.35 us (4%)
    pallas_call x1, Pallas kernels, routed(): pl.pallas_call(functools.partial(kernel, size, nh, apo, columns), out_sha...  104 us
    dot_general x1, matrix products, routed(): lax.dot_general(projectors.reshape(2 * rows_here, nkb), wavefunctions.res...  11.6 us

profile of v1, /device:TPU:0, one launch (start us, length us, event | category | flops | bytes accessed | tf_op | source)
XLA Modules:
  0.0 120.8 jit_solution(10681315115179818967)
XLA Ops:
  0.0 0.0 copy-start
  0.0 11.6 %convolution_bitcast_fusion.term_ref = f32[9216,512]{1,0:T(8,128)} fusion(bf16[2,256,9216]{2,1,0:T(8,128)(2,1)} %param.4, bf16[2,256,512]{2,1,0:T(8,128)(2,1)} %param.5), kind=kOutput, calls=%fused_computation | convolution fusion | flops 4831838208 | bytes 28835840 | tf_op jit(solution)/shard_map/dot_general | solution.py:185
  11.6 0.0 copy-done
  11.6 1.7 %copy.6.coup_ref = f32[128,18,18]{2,1,0:T(8,128)} copy(f32[128,18,18]{0,2,1:T(8,128)S(1)} %copy-done) | data formatting | bytes 331776 | tf_op args[2]
  13.3 103.9 %shard_map.46 = f32[2,16,72,128]{3,2,1,0:T(8,128)} custom-call(s32[512]{0:T(512)} %order_ref.1, f32[9216,512]{1,0:T(8,128)} %convolution_bitcast_fusion.term_ref, f32[128,18,18]{2,1,0:T(8,128)} %copy.6.coup_ref), custom_call_target="tpu_custom_call" | custom-call | tf_op jit(solution)/shard_map/pallas_call | solution.py:199
  117.2 2.0 %fusion = (f32[2304,64]{1,0:T(8,128)S(1)}, f32[2304,64]{1,0:T(8,128)S(1)}) fusion(f32[2304,128]{1,0:T(8,128)} %bitcast.5), kind=kLoop, calls=%fused_computation.2 | loop fusion | bytes 2359296 | tf_op jit(solution)/shard_map/slice | solution.py:223
  119.2 0.3 copy.10
  119.6 0.3 copy.11
  119.9 0.9 broadcast_select_fusion
Async XLA Ops:
  0.0 11.6 %copy-start = (f32[128,18,18]{0,2,1:T(8,128)S(1)}, f32[128,18,18]{0,2,1:T(8,128)}, u32[]{:S(2)}) copy-start(f32[128,18,18]{0,2,1:T(8,128)} %param.6) | copy-start | bytes 497668

commit v2 on v1

--- a/solution.py
+++ b/solution.py
@@ -11,6 +11,7 @@
 MESH = pl.DeviceIdType.MESH
 GROUP = 4
 LANES = 128
+PART = 1152
 
 
 def plain(projectors, wavefunctions, coupling, atom_order):
@@ -36,18 +37,27 @@
     return order, (1 if column % 2 == 0 else -1)
 
 
-def kernel(size, nh, apo, columns, order_ref, term_ref, coup_ref, out_ref, nat, acc, oth, rec, nat_sem, send_sem, recv_sem):
+def divisor(total, most):
+    return max(t for t in range(LANES, most + 1, LANES) if total % t == 0)
+
+
+def kernel(
+    size, nh, apo, columns, order_ref, proj_ref, wave_ref, coup_ref, out_ref, nat, strip, acc, oth, rec, strip_sem, send_sem, recv_sem
+):
     gr, gc = lax.axis_index("gr"), lax.axis_index("gc")
     core, z = lax.rem(gr, 2), gr // 2
     me = {"A": gc // size["B"], "B": lax.rem(gc, size["B"]), "Z": z}
     half = apo // 2
 
-    loads = [
-        pltpu.make_async_copy(term_ref.at[:, pl.ds(i * LANES, LANES)], nat.at[i], nat_sem.at[i])
-        for i in range(size["Z"])
-    ]
-    for load in loads:
-        load.start()
+    slots, _, width = strip.shape
+    strips = proj_ref.shape[1] // width
+
+    def load(number):
+        slot = number % slots
+        return pltpu.make_async_copy(proj_ref.at[:, pl.ds(number * width, width)], strip.at[slot], strip_sem.at[slot])
+
+    for number in range(slots):
+        load(number).start()
 
     def neighbour(dim, way):
         n = size[dim]
@@ -68,10 +78,25 @@
     barrier = pltpu.get_barrier_semaphore()
     for device in greeted:
         pl.semaphore_signal(barrier, inc=1, device_id=device, device_id_type=MESH)
+
+    part = divisor(width, PART)
+    for number in range(strips):
+        load(number).wait()
+
+        def multiply(t, carry, number=number):
+            at = pl.multiple_of(t * part, part)
+            term = lax.dot_general(
+                strip[number % slots, :, pl.ds(at, part)], wave_ref[...],
+                (((0,), (0,)), ((), ())), preferred_element_type=jnp.float32,
+            )
+            for zz in range(size["Z"]):
+                nat[zz, pl.ds(number * width + at, part), :] = term[:, zz * LANES:(zz + 1) * LANES]
+            return carry
+
+        lax.fori_loop(0, width // part, multiply, 0)
+        if number + slots < strips:
+            load(number + slots).start()
     pl.semaphore_wait(barrier, len(greeted))
-
-    for load in loads:
-        load.wait()
 
     def copy(src, dst, column, slot, device):
         return pltpu.make_async_remote_copy(
@@ -162,7 +187,7 @@
             )
         begin(c, n_steps + 1, copy(out_ref.at[core, c], out_ref.at[core, c], c, n_steps + 1, partner))
 
-    lag = [0, 1] + [2 * i + 1 for i in range(1, n_steps + 1)]
+    lag = [0, 1] + [3 * i + 1 for i in range(1, n_steps + 1)]
     for tick in range(columns + lag[-1]):
         for number in reversed(range(n_steps + 2)):
             c = tick - lag[number]
@@ -182,10 +207,7 @@
     columns = apo // 2 // GROUP
     n_steps = sum(size.values()) - 3
     tile = (GROUP * nh, LANES)
-    term = lax.dot_general(
-        projectors.reshape(2 * rows_here, nkb), wavefunctions.reshape(2 * rows_here, bands),
-        (((0,), (0,)), ((), ())), preferred_element_type=jnp.float32,
-    )
+    width = divisor(nkb, 1152)
     acc, rec = [], []
     for c in range(columns):
         n1, n2, n3 = (size[d] for d in path_of(c)[0])
@@ -203,21 +225,25 @@
             pl.BlockSpec(memory_space=pltpu.SMEM),
             pl.BlockSpec(memory_space=pl.ANY),
             pl.BlockSpec(memory_space=pltpu.VMEM),
+            pl.BlockSpec(memory_space=pltpu.VMEM),
         ],
         out_specs=pl.BlockSpec(memory_space=pltpu.VMEM),
         scratch_shapes=[
             pltpu.VMEM((size["Z"], nkb, LANES), jnp.float32),
+            pltpu.VMEM((3, 2 * rows_here, width), projectors.dtype),
             acc,
             list(acc),
             rec,
-            pltpu.SemaphoreType.DMA((size["Z"],)),
+            pltpu.SemaphoreType.DMA((3,)),
             pltpu.SemaphoreType.DMA((columns, n_steps + 2)),
             pltpu.SemaphoreType.DMA((columns, n_steps + 2)),
         ],
         compiler_params=pltpu.CompilerParams(
             collective_id=0, has_side_effects=True, vmem_limit_bytes=67_043_328
         ),
-    )(atom_order, term, coupling)
+    )(
+        atom_order, projectors.reshape(2 * rows_here, nkb), wavefunctions.reshape(2 * rows_here, bands), coupling
+    )
     out = out.reshape(apo * nh, LANES)
     own = LANES // 2
     return jnp.where(lax.rem(lax.axis_index("gr"), 2) == 0, out[:, :own], out[:, own:])

time: 122 us -> 109 us (0.89); the launches traced: 121 us -> 109 us
  matrix products: 11.6 us -> 0 us
    dot_general x1 -> x0, matrix products: 11.6 us -> none  [routed(): lax.dot_general(projectors.reshape(2 * rows_here, nkb), wavefunctions.res...]
    unnamed x5 -> x3, local copies, waits for them, and re-layouts: 2.36 us -> 3.28 us
where the time goes in v2:
time: 109 us
  Pallas kernels  103 us (94%)
  local copies, waits for them, and re-layouts  5.29 us (5%)
    pallas_call x1, Pallas kernels, routed(): pl.pallas_call(functools.partial(kernel, size, nh, apo, columns), out_sha...  103 us
    unnamed x3, local copies, waits for them, and re-layouts  3.28 us

profile of v2, /device:TPU:0, one launch (start us, length us, event | category | flops | bytes accessed | tf_op | source)
XLA Modules:
  0.0 109.2 jit_solution(11070668837434969852)
XLA Ops:
  0.0 2.6 %copy.5.coup_ref = f32[128,18,18]{2,1,0:T(8,128)} copy(f32[128,18,18]{0,2,1:T(8,128)} %param.6) | data formatting | bytes 331776 | tf_op args[2]
  2.6 103.0 %shard_map.46 = f32[2,16,72,128]{3,2,1,0:T(8,128)} custom-call(s32[512]{0:T(512)} %order_ref.1, bf16[512,9216]{1,0:T(8,128)(2,1)} %bitcast.4, bf16[512,512]{1,0:T(8,128)(2,1)} %bitcast.5, f32[128,18,18]{2,1,0:T(8,128)} %copy.5.coup_ref), custom_call_target="tpu_custom_call" | custom-call | tf_op jit(solution)/shard_map/pallas_call | solution.py:221
  105.6 2.0 %fusion = (f32[2304,64]{1,0:T(8,128)S(1)}, f32[2304,64]{1,0:T(8,128)S(1)}) fusion(f32[2304,128]{1,0:T(8,128)} %bitcast.3), kind=kLoop, calls=%fused_computation.1 | loop fusion | bytes 2359296 | tf_op jit(solution)/shard_map/slice | solution.py:249
  107.6 0.3 copy.8
  108.0 0.3 copy.9
  108.3 0.9 broadcast_select_fusion

commit v3 on v2

--- a/solution.py
+++ b/solution.py
@@ -42,7 +42,7 @@
 
 
 def kernel(
-    size, nh, apo, columns, order_ref, proj_ref, wave_ref, coup_ref, out_ref, nat, strip, acc, oth, rec, strip_sem, send_sem, recv_sem
+    size, nh, apo, columns, order_ref, proj_ref, wave_ref, coup_ref, out_ref, fin, mats, nat, strip, acc, oth, rec, strip_sem, send_sem, recv_sem
 ):
     gr, gc = lax.axis_index("gr"), lax.axis_index("gc")
     core, z = lax.rem(gr, 2), gr // 2
@@ -179,22 +179,42 @@
             return
         path, _ = path_of(c)
         mine = tuple(me[d] for d in path)
+        at = pl.ds(c * GROUP * nh, GROUP * nh)
         for i in range(GROUP):
             becp = 2.0 * acc[c][mine + (pl.ds(i * nh, nh), slice(None))]
-            out_ref[core, c, pl.ds(i * nh, nh), :] = jnp.dot(
-                coup_ref[core * half + c * GROUP + i], becp,
+            fin[core, pl.ds((c * GROUP + i) * nh, nh), :] = jnp.dot(
+                mats[:, pl.ds(core * half + c * GROUP + i, 1), :].reshape(nh, nh), becp,
                 precision=lax.Precision.HIGHEST, preferred_element_type=jnp.float32,
             )
-        begin(c, n_steps + 1, copy(out_ref.at[core, c], out_ref.at[core, c], c, n_steps + 1, partner))
+        begin(c, n_steps + 1, copy(fin.at[core, at], fin.at[core, at], c, n_steps + 1, partner))
 
     lag = [0, 1] + [3 * i + 1 for i in range(1, n_steps + 1)]
     for tick in range(columns + lag[-1]):
+        if tick == lag[2]:
+            for i in range(nh):
+                mats[i] = coup_ref[i].T
         for number in reversed(range(n_steps + 2)):
             c = tick - lag[number]
             if 0 <= c < columns:
                 phase(number, c)
+
+    def turn(which):
+        rows = fin.shape[1]
+
+        def body(t, carry):
+            block = fin[which, pl.ds(pl.multiple_of(t * LANES, LANES), LANES), :].T
+            own = LANES // 2
+            at = pl.multiple_of(which * rows + t * LANES, LANES)
+            out_ref[:, pl.ds(at, LANES)] = jnp.where(core == 0, block[:own], block[own:])
+            return carry
+
+        lax.fori_loop(0, rows // LANES, body, 0)
+
+    turn(core)
     for c in range(columns):
         started[c, n_steps + 1].wait_recv()
+    turn(1 - core)
+    for c in range(columns):
         for slot in range(n_steps + 2):
             started[c, slot].wait_send()
 
@@ -220,7 +240,7 @@
         ])
     out = pl.pallas_call(
         functools.partial(kernel, size, nh, apo, columns),
-        out_shape=jax.ShapeDtypeStruct((2, columns) + tile, jnp.float32),
+        out_shape=jax.ShapeDtypeStruct((LANES // 2, apo * nh), jnp.float32),
         in_specs=[
             pl.BlockSpec(memory_space=pltpu.SMEM),
             pl.BlockSpec(memory_space=pl.ANY),
@@ -229,6 +249,8 @@
         ],
         out_specs=pl.BlockSpec(memory_space=pltpu.VMEM),
         scratch_shapes=[
+            pltpu.VMEM((2, apo * nh // 2, LANES), jnp.float32),
+            pltpu.VMEM((nh, apo, nh), jnp.float32),
             pltpu.VMEM((size["Z"], nkb, LANES), jnp.float32),
             pltpu.VMEM((3, 2 * rows_here, width), projectors.dtype),
             acc,
@@ -242,11 +264,10 @@
             collective_id=0, has_side_effects=True, vmem_limit_bytes=67_043_328
         ),
     )(
-        atom_order, projectors.reshape(2 * rows_here, nkb), wavefunctions.reshape(2 * rows_here, bands), coupling
+        atom_order, projectors.reshape(2 * rows_here, nkb), wavefunctions.reshape(2 * rows_here, bands),
+        jnp.transpose(coupling, (1, 2, 0)),
     )
-    out = out.reshape(apo * nh, LANES)
-    own = LANES // 2
-    return jnp.where(lax.rem(lax.axis_index("gr"), 2) == 0, out[:, :own], out[:, own:])
+    return out.T
 
 
 def solution(mesh):
@@ -260,6 +281,7 @@
             and min(size.values()) > 1
             and wavefunctions.shape[2] == size["Z"] * LANES
             and coupling.shape[0] % (2 * GROUP) == 0
+            and projectors.shape[2] % (2 * gc * LANES) == 0
         )
         if fits:
             return routed(size, projectors, wavefunctions, coupling, atom_order)

time: 109 us -> 106 us (0.972)
  local copies, waits for them, and re-layouts: 5.29 us -> 1.92 us
    slice x1 -> x0, local copies, waits for them, and re-layouts: 2.01 us -> none  [routed(): out[:, own:]]
    unnamed x3 -> x1, local copies, waits for them, and re-layouts: 3.28 us -> 1.92 us
where the time goes in v3:
time: 106 us; the launch traced here: 105 us
  Pallas kernels  103 us (97%)
  local copies, waits for them, and re-layouts  1.92 us (2%)
    pallas_call x1, Pallas kernels, routed(): pl.pallas_call(functools.partial(kernel, size, nh, apo, columns), out_sha...  103 us

profile of v3, /device:TPU:0, one launch (start us, length us, event | category | flops | bytes accessed | tf_op | source)
XLA Modules:
  0.0 105.4 jit_solution(7595387038678311632)
XLA Ops:
  0.0 103.4 %shard_map.46 = f32[64,2304]{1,0:T(8,128)} custom-call(s32[512]{0:T(512)} %order_ref.1, bf16[512,9216]{1,0:T(8,128)(2,1)} %bitcast.4, bf16[512,512]{1,0:T(8,128)(2,1)} %bitcast.6, f32[18,18,128]{2,1,0:T(8,128)} %bitcast.7), custom_call_target="tpu_custom_call" | custom-call | tf_op jit(solution)/shard_map/pallas_call | solution.py:241
  103.4 1.9 %copy.6 = f32[2304,64]{0,1:T(8,128)} copy(f32[2304,64]{0,1:T(8,128)} %bitcast.5) | data formatting | bytes 1179648
